TPU v7x, 32 devices: a whole 2x2x4 slice. The times are simulated.
32 devices in a mesh: aux: 16 (over z, y, x), ao: 2 (over core).
Axes of the slice: x: 2, y: 2, z: 4, core: 2. Of those that a mesh axis runs over, the one named last changes fastest.
Arguments:
- ints: bfloat16 [256, 768, 768], P('aux', 'ao'), may hold values from -1.25 to 1.25
- occ_coef: bfloat16 [768, 32], replicated, may hold values from -0.21875 to 0.21875
- vir_coef: bfloat16 [768, 512], P('ao'), may hold values from -0.21875 to 0.21875
- occ_energy: float32 [32], replicated, may hold values from -2 to -0.3
- vir_energy: float32 [512], replicated, may hold values from 0.3 to 3
Outputs:
- density: float32 [32, 512, 512], P('aux', 'ao')
All inputs are finite; a program needn't handle non-finite values.
Results may differ from a plain program's by a relative error of at most 0.0065.
Values may be sent and summed in bfloat16 or wider, within the bound.
A program may use at most 128 MiB of HBM per device.

v0:
```python
import functools

import jax
import jax.numpy as jnp
from jax import lax
from jax.experimental import pallas as pl
from jax.experimental.pallas import tpu as pltpu
from jax.sharding import PartitionSpec as P

CYCLE = 4
MESH = pl.DeviceIdType.MESH
NT = (((1,), (1,)), ((), ()))


def offset_of(slot):
    size = CYCLE + 1 - (slot + 1) // 2
    return 0 if slot == 0 else (size if slot % 2 else -size)


def pairs_kernel(
    aux_count, share, own_ref, occ_ref, vir_row_ref, vir_col_ref, out_ref,
    slots, own_t, vis_t, vir_pairs, amp, mix, acc, outgoing, incoming,
    send_sems, recv_sems, swap_sems,
):
    me = lax.axis_index("aux")
    core = lax.axis_index("ao")
    other = 1 - core
    block, _, nvir = own_ref.shape
    half = nvir // 2
    slot_count = 2 * CYCLE + 1

    barrier = pltpu.get_barrier_semaphore()
    for slot in range(1, slot_count):
        target = lax.rem(me + aux_count + offset_of(slot), aux_count)
        pl.semaphore_signal(barrier, inc=1, device_id=(target, core), device_id_type=MESH)
    pl.semaphore_signal(barrier, inc=1, device_id=(me, other), device_id_type=MESH)
    pl.semaphore_wait(barrier, slot_count)

    piece = own_ref.at[pl.ds(core * share, share)]
    sends = []
    for slot in range(1, slot_count):
        target = lax.rem(me + aux_count - offset_of(slot), aux_count)
        sends.append(
            pltpu.make_async_remote_copy(
                src_ref=piece,
                dst_ref=slots.at[slot],
                send_sem=send_sems.at[slot],
                recv_sem=recv_sems.at[slot],
                device_id=(target, core),
                device_id_type=MESH,
            )
        )
        sends[-1].start()
    pltpu.make_async_copy(piece, slots.at[0], recv_sems.at[0]).start()

    for i in range(block):
        own_t[i] = own_ref[i].T
    vir_pairs[...] = vir_col_ref[...] + vir_row_ref[...]
    acc[...] = jnp.zeros_like(acc)

    def visit(slot, carry):
        size = CYCLE + 1 - lax.div(slot + 1, 2)
        signed = jnp.where(lax.rem(slot, 2) == 1, size, -size)
        offset = jnp.where(slot == 0, 0, signed)
        owner = lax.rem(me + aux_count + offset, aux_count)
        pltpu.make_async_copy(slots.at[slot], slots.at[slot], recv_sems.at[slot]).wait()
        for s in range(share):
            pair_energy = occ_ref[owner * block + core * share + s]
            visitor = slots[slot, s]
            vis_t[...] = visitor.T
            for i in range(block):
                energy = occ_ref[me * block + i] + pair_energy
                for t in range(2):
                    rows = slice(t * half, (t + 1) * half)
                    direct = jnp.dot(own_t[i, rows], visitor, preferred_element_type=jnp.float32)
                    swapped = jnp.dot(vis_t[rows], own_ref[i], preferred_element_type=jnp.float32)
                    inverse = 1.0 / (energy - vir_pairs[rows])
                    amp[i, rows] = (direct * inverse).astype(jnp.bfloat16)
                    mix[i, rows] = ((2.0 * direct - swapped) * inverse).astype(jnp.bfloat16)
                acc[i] += lax.dot_general(amp[i], mix[i], NT, preferred_element_type=jnp.float32)
        return carry

    lax.fori_loop(0, slot_count, visit, 0)

    outgoing[...] = acc[:, pl.ds(pl.multiple_of(other * half, half), half)].astype(jnp.bfloat16)
    swap = pltpu.make_async_remote_copy(
        src_ref=outgoing,
        dst_ref=incoming,
        send_sem=swap_sems.at[0],
        recv_sem=swap_sems.at[1],
        device_id=(me, other),
        device_id_type=MESH,
    )
    swap.start()
    for send in sends:
        send.wait_send()
    swap.wait()
    kept = acc[:, pl.ds(pl.multiple_of(core * half, half), half)]
    out_ref[...] = kept + incoming[...].astype(jnp.float32)


def pair_densities(own_block, occ_energy, vir_energy, aux_count, share):
    block, naux, nvir = own_block.shape
    half = nvir // 2
    slot_count = 2 * CYCLE + 1
    vmem = pl.BlockSpec(memory_space=pltpu.VMEM)
    return pl.pallas_call(
        functools.partial(pairs_kernel, aux_count, share),
        out_shape=jax.ShapeDtypeStruct((block, half, nvir), jnp.float32),
        in_specs=[vmem, pl.BlockSpec(memory_space=pltpu.SMEM), vmem, vmem],
        out_specs=vmem,
        scratch_shapes=[
            pltpu.VMEM((slot_count, share, naux, nvir), jnp.bfloat16),
            pltpu.VMEM((block, nvir, naux), jnp.bfloat16),
            pltpu.VMEM((nvir, naux), jnp.bfloat16),
            pltpu.VMEM((nvir, nvir), jnp.float32),
            pltpu.VMEM((block, nvir, nvir), jnp.bfloat16),
            pltpu.VMEM((block, nvir, nvir), jnp.bfloat16),
            pltpu.VMEM((block, nvir, nvir), jnp.float32),
            pltpu.VMEM((block, half, nvir), jnp.bfloat16),
            pltpu.VMEM((block, half, nvir), jnp.bfloat16),
            pltpu.SemaphoreType.DMA((slot_count,)),
            pltpu.SemaphoreType.DMA((slot_count,)),
            pltpu.SemaphoreType.DMA((2,)),
        ],
        compiler_params=pltpu.CompilerParams(collective_id=0, has_side_effects=True, vmem_limit_bytes=48 * 2**20),
    )(own_block, occ_energy, vir_energy[None, :], vir_energy[:, None])


def shards(ints, occ_coef, vir_coef, occ_energy, vir_energy):
    core = lax.axis_index("ao")
    aux_count = lax.axis_size("aux")
    ao_count = lax.axis_size("ao")
    share = occ_coef.shape[1] // aux_count // ao_count
    half = vir_coef.shape[1] // ao_count
    half_ints = jnp.einsum(
        "qmn,ni->qmi", ints, occ_coef, preferred_element_type=jnp.float32
    ).astype(jnp.bfloat16)
    partial_sum = jnp.einsum("qmi,ma->qia", half_ints, vir_coef, preferred_element_type=jnp.float32)
    given = lax.dynamic_slice_in_dim(partial_sum, (1 - core) * half, half, 2).astype(jnp.bfloat16)
    taken = lax.ppermute(given, "ao", [(0, 1), (1, 0)])
    kept = lax.dynamic_slice_in_dim(partial_sum, core * half, half, 2)
    summed = (kept + taken.astype(jnp.float32)).astype(jnp.bfloat16)
    grouped = lax.all_to_all(summed, "aux", split_axis=1, concat_axis=0, tiled=True)
    own_block = lax.all_gather(grouped, "ao", axis=2, tiled=True)
    return pair_densities(
        jnp.swapaxes(own_block, 0, 1), occ_energy, vir_energy, aux_count, share
    )


def solution(mesh):
    return jax.shard_map(
        shards,
        mesh=mesh,
        in_specs=(P("aux", "ao", None), P(), P("ao", None), P(), P()),
        out_specs=P("aux", "ao", None),
        check_vma=False,
    )
```

profile of v0, /device:TPU:0, one launch (start us, length us, event | category | flops | bytes accessed | tf_op | source)
XLA Modules:
  0.0 79.2 jit_solution(78880973750580334)
XLA Ops:
  0.0 0.0 copy-start
  0.0 0.0 copy-start.1
  0.0 0.0 copy-start.2
  0.0 1.0 %copy-done = bf16[384,512]{1,0:T(8,128)(2,1)S(1)} copy-done((bf16[384,512]{1,0:T(8,128)(2,1)S(1)}, bf16[384,512]{1,0:T(8,128)(2,1)}, u32[]{:S(2)}) %copy-start) | copy-done | bytes 393240
  1.0 6.8 %fusion = f32[16,32,512]{2,1,0:T(8,128)S(1)} fusion(bf16[16,384,768]{2,1,0:T(8,128)(2,1)} %param.5, bf16[384,512]{1,0:T(8,128)(2,1)S(1)} %copy-done, bf16[768,32]{0,1:T(8,128)(2,1)} %param.6), kind=kOutput, calls=%fused_computation.1 | convolution fusion | flops 503513088 | bytes 10928128 | tf_op jit(solution)/shard_map/qmi,ma->qia/dot_general | solution.py:139
  7.9 0.6 collective-permute-start
  8.5 1.2 %collective-permute-done = bf16[16,32,256]{2,1,0:T(8,128)(2,1)S(1)} collective-permute-done((bf16[16,32,256]{2,1,0:T(8,128)(2,1)S(1)}, bf16[16,32,256]{2,1,0:T(8,128)(2,1)S(1)}, u32[]{:S(2)}, u32[]{:S(2)}) %collective-permute-start) | collective-permute-done | bytes 262176 | tf_op jit(solution)/shard_map/ppermute | solution.py:141
  9.6 0.1 add_convert_fusion
  9.7 0.9 %copy.9 = bf16[16,32,256]{2,0,1:T(8,128)(2,1)} copy(bf16[16,32,256]{2,1,0:T(8,128)(2,1)S(1)} %add_convert_fusion) | data formatting | bytes 524288 | tf_op jit(solution)/shard_map/convert_element_type | solution.py:143
  10.6 8.2 %all-to-all-start = ((bf16[16,32,256]{2,0,1:T(8,128)(2,1)}), bf16[16,32,256]{2,0,1:T(8,128)(2,1)S(1)}, u32[]{:S(2)}, u32[]{:S(2)}) async-start(bf16[16,32,256]{2,0,1:T(8,128)(2,1)} %copy.9), calls=%async_computation | async-start | bytes 524288 | tf_op jit(solution)/shard_map/all_to_all | solution.py:144
  18.8 0.0 copy-done.1
  18.8 0.1 copy.11.vir_col_ref
  19.0 10.0 %all-to-all-done = bf16[16,32,256]{2,0,1:T(8,128)(2,1)S(1)} async-done(((bf16[16,32,256]{2,0,1:T(8,128)(2,1)}), bf16[16,32,256]{2,0,1:T(8,128)(2,1)S(1)}, u32[]{:S(2)}, u32[]{:S(2)}) %all-to-all-start) | async-done | bytes 262176 | tf_op jit(solution)/shard_map/all_to_all | solution.py:144
  29.0 2.2 %all_gather.3 = bf16[256,2,512]{2,0,1:T(8,128)(2,1)S(1)} all-gather(bf16[256,2,256]{2,0,1:T(8,128)(2,1)S(1)} %bitcast.18), channel_id=1, replica_groups=mesh['aux'=16,'ao'=2] {'ao'}, dimensions={2}, use_global_device_ids=true | all-gather | bytes 786432 | tf_op jit(solution)/shard_map/all_gather | solution.py:145
  31.2 0.0 copy-done.2
  31.2 47.0 %shard_map.55 = f32[2,256,512]{2,1,0:T(8,128)S(1)} custom-call(bf16[2,256,512]{2,1,0:T(8,128)(2,1)S(1)} %bitcast.15, f32[32]{0:T(128)S(1)} %copy-done.2, f32[1,512]{1,0:T(1,128)S(1)} %bitcast.17, f32[512,1]{1,0:T(8,128)S(1)} %copy.11.vir_col_ref), custom_call_target="tpu_custom_call" | custom-call | tf_op jit(solution)/shard_map/pallas_call | solution.py:107
  78.2 1.0 %copy.13 = f32[2,256,512]{2,1,0:T(8,128)} copy(f32[2,256,512]{2,1,0:T(8,128)S(1)} %shard_map.55) | data formatting | bytes 2097152
  (2 shorter events, 0.1 us)
Async XLA Ops:
  0.0 1.0 %copy-start = (bf16[384,512]{1,0:T(8,128)(2,1)S(1)}, bf16[384,512]{1,0:T(8,128)(2,1)}, u32[]{:S(2)}) copy-start(bf16[384,512]{1,0:T(8,128)(2,1)} %param.7) | copy-start | bytes 1179652
  0.0 18.8 %copy-start.1 = (f32[512]{0:T(512)S(1)}, f32[512]{0:T(512)}, u32[]{:S(2)}) copy-start(f32[512]{0:T(512)} %param.9) | copy-start | bytes 6148
  0.0 31.2 %copy-start.2 = (f32[32]{0:T(128)S(1)}, f32[32]{0:T(128)}, u32[]{:S(2)}) copy-start(f32[32]{0:T(128)} %occ_ref.1) | copy-start | bytes 388
  7.9 1.7 %collective-permute-start = (bf16[16,32,256]{2,1,0:T(8,128)(2,1)S(1)}, bf16[16,32,256]{2,1,0:T(8,128)(2,1)S(1)}, u32[]{:S(2)}, u32[]{:S(2)}) collective-permute-start(bf16[16,32,256]{2,1,0:T(8,128)(2,1)S(1)} %dynamic-slice_convert_fusion), channel_id=1, source_target_pairs={{0,1},{1,0},{2,3},{3,2},{4,5},{5,4},{6,7},{7,6},{8,9},{9,8},{10,11... | collective-permute-start | bytes 786440 | tf_op jit(solution)/shard_map/ppermute | solution.py:141
  10.6 18.4 %all-to-all-start = ((bf16[16,32,256]{2,0,1:T(8,128)(2,1)}), bf16[16,32,256]{2,0,1:T(8,128)(2,1)S(1)}, u32[]{:S(2)}, u32[]{:S(2)}) async-start(bf16[16,32,256]{2,0,1:T(8,128)(2,1)} %copy.9), calls=%async_computation | async-start | bytes 524288 | tf_op jit(solution)/shard_map/all_to_all | solution.py:144
where the time goes:
time: 79.4 us; the launch traced here: 79.2 us
  Pallas kernels  47 us (59%)
  waiting for transfers between devices  11.2 us (14%)
  starting transfers between devices  8.78 us (11%)
  matrix products  6.84 us (9%)
  local copies, waits for them, and re-layouts  3.03 us (4%)
  blocking collectives  2.18 us (3%)
    pallas_call x1, Pallas kernels, pair_densities(): pl.pallas_call(functools.partial(pairs_kernel, aux_count, share), out_sha...  47 us
    all_to_all x1, waiting for transfers between devices, shards(): lax.all_to_all(summed, 'aux', split_axis=1, concat_axis=0, tiled=True)  10 us
    all_to_all x1, starting transfers between devices, shards(): lax.all_to_all(summed, 'aux', split_axis=1, concat_axis=0, tiled=True)  8.22 us
    dot_general x1, matrix products, shards(): jnp.einsum('qmi,ma->qia', half_ints, vir_coef, preferred_element_type=jnp...  6.84 us
    all_gather x1, blocking collectives, shards(): own_block = lax.all_gather(grouped, 'ao', axis=2, tiled=True)  2.18 us
    unnamed x7, local copies, waits for them, and re-layouts  1.97 us
  transfers between devices with their start and end apart: 2, of which 2 were waited for; matrix products, arithmetic and copies ran while one was open for 0% of the time, Pallas kernels for 0%

commit v1 on v0

--- a/solution.py
+++ b/solution.py
@@ -12,9 +12,18 @@
 NT = (((1,), (1,)), ((), ()))
 
 
-def offset_of(slot):
-    size = CYCLE + 1 - (slot + 1) // 2
-    return 0 if slot == 0 else (size if slot % 2 else -size)
+def places(me, aux_count):
+    layers = aux_count // CYCLE
+    layer, place = lax.div(me, CYCLE), lax.rem(me, CYCLE)
+    column, row = lax.rem(place, 2), lax.div(place, 2)
+    base = layer * CYCLE
+    beside = base + place + 1 - 2 * column
+    along = base + place + 2 - 4 * row
+    across = base + CYCLE - 1 - place
+    above = lax.rem(me + CYCLE, aux_count)
+    below = lax.rem(me + aux_count - CYCLE, aux_count)
+    last = jnp.where(layer == layers - 1, 1, 0)
+    return column, row, beside, along, across, above, below, last
 
 
 def pairs_kernel(
@@ -28,42 +37,81 @@
     block, _, nvir = own_ref.shape
     half = nvir // 2
     slot_count = 2 * CYCLE + 1
+    column, row, beside, along, across, above, below, last = places(me, aux_count)
 
     barrier = pltpu.get_barrier_semaphore()
-    for slot in range(1, slot_count):
-        target = lax.rem(me + aux_count + offset_of(slot), aux_count)
+    for target in (beside, along, across, above, below):
         pl.semaphore_signal(barrier, inc=1, device_id=(target, core), device_id_type=MESH)
     pl.semaphore_signal(barrier, inc=1, device_id=(me, other), device_id_type=MESH)
-    pl.semaphore_wait(barrier, slot_count)
+    pl.semaphore_wait(barrier, 6)
+
+    def remote(source, slot, target):
+        return pltpu.make_async_remote_copy(
+            src_ref=source,
+            dst_ref=slots.at[slot],
+            send_sem=send_sems.at[slot],
+            recv_sem=recv_sems.at[slot],
+            device_id=(target, core),
+            device_id_type=MESH,
+        )
+
+    def arrived(slot):
+        pltpu.make_async_copy(slots.at[slot], slots.at[slot], recv_sems.at[slot]).wait()
 
     piece = own_ref.at[pl.ds(core * share, share)]
-    sends = []
-    for slot in range(1, slot_count):
-        target = lax.rem(me + aux_count - offset_of(slot), aux_count)
-        sends.append(
-            pltpu.make_async_remote_copy(
-                src_ref=piece,
-                dst_ref=slots.at[slot],
-                send_sem=send_sems.at[slot],
-                recv_sem=recv_sems.at[slot],
-                device_id=(target, core),
-                device_id_type=MESH,
-            )
-        )
-        sends[-1].start()
+    first = jnp.where(last == 1, below, above)
+    second = jnp.where(last == 1, above, below)
+    remote(piece, 1, beside).start()
+    remote(piece, 2, along).start()
+    remote(piece, 5 - last, first).start()
+    remote(piece, 3, across).start()
+    remote(piece, 4 + last, second).start()
     pltpu.make_async_copy(piece, slots.at[0], recv_sems.at[0]).start()
+    beside_source, along_source = 4 + column, 4 + row
+    beyond = jnp.where(row == 0, above, below)
 
     for i in range(block):
         own_t[i] = own_ref[i].T
     vir_pairs[...] = vir_col_ref[...] + vir_row_ref[...]
     acc[...] = jnp.zeros_like(acc)
 
-    def visit(slot, carry):
-        size = CYCLE + 1 - lax.div(slot + 1, 2)
-        signed = jnp.where(lax.rem(slot, 2) == 1, size, -size)
-        offset = jnp.where(slot == 0, 0, signed)
-        owner = lax.rem(me + aux_count + offset, aux_count)
-        pltpu.make_async_copy(slots.at[slot], slots.at[slot], recv_sems.at[slot]).wait()
+    near, far = 4 + last, 5 - last
+
+    def forward(source):
+        @pl.when(beside_source == source)
+        def _():
+            remote(slots.at[source], 6, beside).start()
+
+        @pl.when(along_source == source)
+        def _():
+            remote(slots.at[source], 7, along).start()
+
+    def visit(step, carry):
+        slot = jnp.where(step == 1, near, jnp.where(step == 4, far, jnp.where(step == 5, 3, step)))
+        slot = jnp.where(step == 2, 1, jnp.where(step == 3, 2, slot))
+
+        @pl.when(step != 5)
+        def _():
+            arrived(slot)
+
+        @pl.when(step == 1)
+        def _():
+            forward(near)
+
+        @pl.when(step == 4)
+        def _():
+            forward(far)
+            arrived(3)
+            remote(slots.at[3], 8, beyond).start()
+
+        to_owner = jnp.where(slot == 0, me, jnp.where(slot == 1, beside, jnp.where(slot == 2, along, across)))
+        from_beside = jnp.where(column == 1, beside + CYCLE, beside + aux_count - CYCLE)
+        from_along = jnp.where(row == 1, along + CYCLE, along + aux_count - CYCLE)
+        from_beyond = jnp.where(row == 1, across + CYCLE, across + aux_count - CYCLE)
+        forwarded = jnp.where(slot == 6, from_beside, jnp.where(slot == 7, from_along, from_beyond))
+        forwarded = lax.rem(forwarded, aux_count)
+        stacked = jnp.where(slot == 4, above, below)
+        owner = jnp.where(slot < 4, to_owner, jnp.where(slot < 6, stacked, forwarded))
         for s in range(share):
             pair_energy = occ_ref[owner * block + core * share + s]
             visitor = slots[slot, s]
@@ -92,8 +140,8 @@
         device_id_type=MESH,
     )
     swap.start()
-    for send in sends:
-        send.wait_send()
+    for slot in range(1, slot_count):
+        remote(piece, slot, beside).wait_send()
     swap.wait()
     kept = acc[:, pl.ds(pl.multiple_of(core * half, half), half)]
     out_ref[...] = kept + incoming[...].astype(jnp.float32)

time: 79.4 us -> 61.5 us (0.77)
  Pallas kernels: 47 us -> 29 us
    pallas_call x1, Pallas kernels: 47 us -> 29 us  [pair_densities(): pl.pallas_call(functools.partial(pairs_kernel, aux_count, share), out_sha...]
where the time goes in v1:
time: 61.5 us; the launch traced here: 61.2 us
  Pallas kernels  29 us (47%)
  waiting for transfers between devices  11.2 us (18%)
  starting transfers between devices  8.78 us (14%)
  matrix products  6.84 us (11%)
  local copies, waits for them, and re-layouts  3.03 us (5%)
  blocking collectives  2.18 us (4%)
    pallas_call x1, Pallas kernels, pair_densities(): pl.pallas_call(functools.partial(pairs_kernel, aux_count, share), out_sha...  29 us
    all_to_all x1, waiting for transfers between devices, shards(): lax.all_to_all(summed, 'aux', split_axis=1, concat_axis=0, tiled=True)  10 us
    all_to_all x1, starting transfers between devices, shards(): lax.all_to_all(summed, 'aux', split_axis=1, concat_axis=0, tiled=True)  8.22 us
    dot_general x1, matrix products, shards(): jnp.einsum('qmi,ma->qia', half_ints, vir_coef, preferred_element_type=jnp...  6.84 us
    all_gather x1, blocking collectives, shards(): own_block = lax.all_gather(grouped, 'ao', axis=2, tiled=True)  2.18 us
    unnamed x7, local copies, waits for them, and re-layouts  1.97 us
  transfers between devices with their start and end apart: 2, of which 2 were waited for; matrix products, arithmetic and copies ran while one was open for 0% of the time, Pallas kernels for 0%

profile of v1, /device:TPU:0, one launch (start us, length us, event | category | flops | bytes accessed | tf_op | source)
XLA Modules:
  0.0 61.2 jit_solution(12739885999340243348)
XLA Ops:
  0.0 0.0 copy-start
  0.0 0.0 copy-start.1
  0.0 0.0 copy-start.2
  0.0 1.0 %copy-done = bf16[384,512]{1,0:T(8,128)(2,1)S(1)} copy-done((bf16[384,512]{1,0:T(8,128)(2,1)S(1)}, bf16[384,512]{1,0:T(8,128)(2,1)}, u32[]{:S(2)}) %copy-start) | copy-done | bytes 393240
  1.0 6.8 %fusion = f32[16,32,512]{2,1,0:T(8,128)S(1)} fusion(bf16[16,384,768]{2,1,0:T(8,128)(2,1)} %param.5, bf16[384,512]{1,0:T(8,128)(2,1)S(1)} %copy-done, bf16[768,32]{0,1:T(8,128)(2,1)} %param.6), kind=kOutput, calls=%fused_computation.1 | convolution fusion | flops 503513088 | bytes 10928128 | tf_op jit(solution)/shard_map/qmi,ma->qia/dot_general | solution.py:187
  7.9 0.6 collective-permute-start
  8.5 1.2 %collective-permute-done = bf16[16,32,256]{2,1,0:T(8,128)(2,1)S(1)} collective-permute-done((bf16[16,32,256]{2,1,0:T(8,128)(2,1)S(1)}, bf16[16,32,256]{2,1,0:T(8,128)(2,1)S(1)}, u32[]{:S(2)}, u32[]{:S(2)}) %collective-permute-start) | collective-permute-done | bytes 262176 | tf_op jit(solution)/shard_map/ppermute | solution.py:189
  9.6 0.1 add_convert_fusion
  9.7 0.9 %copy.9 = bf16[16,32,256]{2,0,1:T(8,128)(2,1)} copy(bf16[16,32,256]{2,1,0:T(8,128)(2,1)S(1)} %add_convert_fusion) | data formatting | bytes 524288 | tf_op jit(solution)/shard_map/convert_element_type | solution.py:191
  10.6 8.2 %all-to-all-start = ((bf16[16,32,256]{2,0,1:T(8,128)(2,1)}), bf16[16,32,256]{2,0,1:T(8,128)(2,1)S(1)}, u32[]{:S(2)}, u32[]{:S(2)}) async-start(bf16[16,32,256]{2,0,1:T(8,128)(2,1)} %copy.9), calls=%async_computation | async-start | bytes 524288 | tf_op jit(solution)/shard_map/all_to_all | solution.py:192
  18.8 0.0 copy-done.1
  18.8 0.1 copy.11.vir_col_ref
  19.0 10.0 %all-to-all-done = bf16[16,32,256]{2,0,1:T(8,128)(2,1)S(1)} async-done(((bf16[16,32,256]{2,0,1:T(8,128)(2,1)}), bf16[16,32,256]{2,0,1:T(8,128)(2,1)S(1)}, u32[]{:S(2)}, u32[]{:S(2)}) %all-to-all-start) | async-done | bytes 262176 | tf_op jit(solution)/shard_map/all_to_all | solution.py:192
  29.0 2.2 %all_gather.3 = bf16[256,2,512]{2,0,1:T(8,128)(2,1)S(1)} all-gather(bf16[256,2,256]{2,0,1:T(8,128)(2,1)S(1)} %bitcast.18), channel_id=1, replica_groups=mesh['aux'=16,'ao'=2] {'ao'}, dimensions={2}, use_global_device_ids=true | all-gather | bytes 786432 | tf_op jit(solution)/shard_map/all_gather | solution.py:193
  31.2 0.0 copy-done.2
  31.2 29.0 %shard_map.55 = f32[2,256,512]{2,1,0:T(8,128)S(1)} custom-call(bf16[2,256,512]{2,1,0:T(8,128)(2,1)S(1)} %bitcast.15, f32[32]{0:T(128)S(1)} %copy-done.2, f32[1,512]{1,0:T(1,128)S(1)} %bitcast.17, f32[512,1]{1,0:T(8,128)S(1)} %copy.11.vir_col_ref), custom_call_target="tpu_custom_call" | custom-call | tf_op jit(solution)/shard_map/pallas_call | solution.py:155
  60.2 1.0 %copy.13 = f32[2,256,512]{2,1,0:T(8,128)} copy(f32[2,256,512]{2,1,0:T(8,128)S(1)} %shard_map.55) | data formatting | bytes 2097152
  (2 shorter events, 0.1 us)
Async XLA Ops:
  0.0 1.0 %copy-start = (bf16[384,512]{1,0:T(8,128)(2,1)S(1)}, bf16[384,512]{1,0:T(8,128)(2,1)}, u32[]{:S(2)}) copy-start(bf16[384,512]{1,0:T(8,128)(2,1)} %param.7) | copy-start | bytes 1179652
  0.0 18.8 %copy-start.1 = (f32[512]{0:T(512)S(1)}, f32[512]{0:T(512)}, u32[]{:S(2)}) copy-start(f32[512]{0:T(512)} %param.9) | copy-start | bytes 6148
  0.0 31.2 %copy-start.2 = (f32[32]{0:T(128)S(1)}, f32[32]{0:T(128)}, u32[]{:S(2)}) copy-start(f32[32]{0:T(128)} %occ_ref.1) | copy-start | bytes 388
  7.9 1.7 %collective-permute-start = (bf16[16,32,256]{2,1,0:T(8,128)(2,1)S(1)}, bf16[16,32,256]{2,1,0:T(8,128)(2,1)S(1)}, u32[]{:S(2)}, u32[]{:S(2)}) collective-permute-start(bf16[16,32,256]{2,1,0:T(8,128)(2,1)S(1)} %dynamic-slice_convert_fusion), channel_id=1, source_target_pairs={{0,1},{1,0},{2,3},{3,2},{4,5},{5,4},{6,7},{7,6},{8,9},{9,8},{10,11... | collective-permute-start | bytes 786440 | tf_op jit(solution)/shard_map/ppermute | solution.py:189
  10.6 18.4 %all-to-all-start = ((bf16[16,32,256]{2,0,1:T(8,128)(2,1)}), bf16[16,32,256]{2,0,1:T(8,128)(2,1)S(1)}, u32[]{:S(2)}, u32[]{:S(2)}) async-start(bf16[16,32,256]{2,0,1:T(8,128)(2,1)} %copy.9), calls=%async_computation | async-start | bytes 524288 | tf_op jit(solution)/shard_map/all_to_all | solution.py:192

commit v2 on v1

v2 whole, which is shorter than its diff:
```python
import functools

import jax
import jax.numpy as jnp
from jax import lax
from jax.experimental import pallas as pl
from jax.experimental.pallas import tpu as pltpu
from jax.sharding import PartitionSpec as P

CYCLE = 4
MESH = pl.DeviceIdType.MESH
NT = (((1,), (1,)), ((), ()))


def places(me, aux_count):
    layers = aux_count // CYCLE
    layer, place = lax.div(me, CYCLE), lax.rem(me, CYCLE)
    column, row = lax.rem(place, 2), lax.div(place, 2)
    base = layer * CYCLE
    beside = base + place + 1 - 2 * column
    along = base + place + 2 - 4 * row
    across = base + CYCLE - 1 - place
    above = lax.rem(me + CYCLE, aux_count)
    below = lax.rem(me + aux_count - CYCLE, aux_count)
    last = jnp.where(layer == layers - 1, 1, 0)
    return column, row, beside, along, across, above, below, last


def density_kernel(
    aux_count, share, ints_ref, occ_ref, vir_ref, occ_energy_ref, vir_energy_ref, out_ref,
    ints, occ_t, vir, occ_energy, vir_energy, half_ints, given, taken, kept, outbox, own,
    slots, own_t, vis_t, vir_pairs, amp, mix, acc, outgoing, incoming,
    load_sems, input_sems, give_sems, take_sems, spread_sems, join_sems,
    send_sems, recv_sems, swap_sems,
):
    me = lax.axis_index("aux")
    core = lax.axis_index("ao")
    other = 1 - core
    block, naux, nvir = own.shape
    groups, rows_in_group, nao = ints.shape
    chunks, norb, depth, half = outbox.shape
    part = half_ints.shape[2]
    held = chunks * depth
    slot_count = 2 * CYCLE + 1
    column, row, beside, along, across, above, below, last = places(me, aux_count)
    f32, bf16 = jnp.float32, jnp.bfloat16

    inputs = [
        pltpu.make_async_copy(source, target, input_sems.at[at])
        for at, (source, target) in enumerate(
            ((occ_ref, occ_t), (vir_ref, vir), (vir_energy_ref, vir_energy), (occ_energy_ref, occ_energy))
        )
    ]
    loads = [
        pltpu.make_async_copy(
            ints_ref.at[pl.ds(group * rows_in_group, rows_in_group)], ints.at[group], load_sems.at[group]
        )
        for group in range(groups)
    ]
    inputs[0].start()
    loads[0].start()
    for copy in inputs[1:] + loads[1:]:
        copy.start()

    barrier = pltpu.get_barrier_semaphore()

    def greet(step, carry):
        target = lax.rem(me + step, aux_count)
        pl.semaphore_signal(barrier, inc=1, device_id=(target, core), device_id_type=MESH)
        return carry

    lax.fori_loop(1, aux_count, greet, 0)
    pl.semaphore_signal(barrier, inc=1, device_id=(me, other), device_id_type=MESH)

    inputs[0].wait()
    occ = occ_t[...].T
    acc[...] = jnp.zeros_like(acc)
    inputs[1].wait()
    mine = pl.ds(pl.multiple_of(core * half, half), half)
    theirs = pl.ds(pl.multiple_of(other * half, half), half)
    to_row = lax.broadcasted_iota(jnp.int32, (norb * depth, norb * depth), 0)
    from_row = lax.broadcasted_iota(jnp.int32, (norb * depth, norb * depth), 1)
    order = jnp.where(from_row == lax.rem(to_row, depth) * norb + lax.div(to_row, depth), 1.0, 0.0).astype(bf16)

    def give(chunk):
        return pltpu.make_async_remote_copy(
            src_ref=given.at[chunk],
            dst_ref=taken.at[chunk],
            send_sem=give_sems.at[chunk],
            recv_sem=take_sems.at[chunk],
            device_id=(me, other),
            device_id_type=MESH,
        )

    def spread(chunk):
        give(chunk).wait_recv()
        total = kept[chunk] + taken[chunk].astype(f32)
        outbox[chunk] = total.astype(bf16).reshape(norb, depth, half)
        place = pl.ds(pl.multiple_of(me * held + chunk * depth, depth), depth)

        def send(step, carry):
            target = lax.rem(me + step, aux_count)
            pltpu.make_async_remote_copy(
                src_ref=outbox.at[chunk, pl.ds(target * block, block)],
                dst_ref=own.at[:, place, mine],
                send_sem=spread_sems.at[0],
                recv_sem=spread_sems.at[1],
                device_id=(target, core),
                device_id_type=MESH,
            ).start()
            return carry

        lax.fori_loop(1, aux_count, send, 0)
        pltpu.make_async_copy(
            outbox.at[chunk, pl.ds(me * block, block)], own.at[:, place, mine], spread_sems.at[1]
        ).start()

    in_chunk = groups // chunks
    in_group = rows_in_group // part
    cut = rows_in_group // 2
    for group in range(groups):
        chunk = group // in_chunk
        loads[group].wait()
        for piece in range(2):
            product = jnp.dot(ints[group, piece * cut : (piece + 1) * cut], occ, preferred_element_type=f32).astype(bf16)
            for q in range(in_group // 2):
                at = ((group % in_chunk) * in_group + piece * (in_group // 2) + q) * norb
                half_ints[chunk, at : at + norb] = product[q * part : (q + 1) * part].T
        if group % in_chunk == in_chunk - 1:
            ordered = jnp.dot(order, half_ints[chunk], preferred_element_type=f32).astype(bf16)
            given[chunk] = jnp.dot(ordered, vir[:, theirs], preferred_element_type=f32).astype(bf16)
            if chunk == 0:
                pl.semaphore_wait(barrier, aux_count)
            give(chunk).start()
            kept[chunk] = jnp.dot(ordered, vir[:, mine], preferred_element_type=f32)
        elif chunk > 0:
            spread(chunk - 1)
    spread(chunks - 1)

    inputs[2].wait()
    inputs[3].wait()
    lanes = 128
    column_energy = jnp.broadcast_to(vir_energy[...], (lanes, nvir)).T
    vir_pairs[...] = jnp.concatenate([column_energy] * (nvir // lanes), axis=1) + vir_energy[...]

    def remote(source, slot, target, columns=slice(None)):
        return pltpu.make_async_remote_copy(
            src_ref=source.at[:, :, columns],
            dst_ref=slots.at[slot, :, :, columns],
            send_sem=send_sems.at[slot],
            recv_sem=recv_sems.at[slot],
            device_id=(target, core),
            device_id_type=MESH,
        )

    def arrived(slot):
        pltpu.make_async_copy(slots.at[slot], slots.at[slot], recv_sems.at[slot]).wait()

    def join(orbital, at):
        half_block = own.at[pl.ds(orbital * share, share), :, mine]
        return pltpu.make_async_remote_copy(
            src_ref=half_block,
            dst_ref=half_block,
            send_sem=join_sems.at[0, at],
            recv_sem=join_sems.at[1, at],
            device_id=(me, other),
            device_id_type=MESH,
        )

    own_half = own.at[:, :, mine]
    pltpu.make_async_copy(own_half, own_half, spread_sems.at[1]).wait()
    join(other, 0).start()
    piece = own.at[pl.ds(core * share, share)]
    first = jnp.where(last == 1, below, above)
    second = jnp.where(last == 1, above, below)
    for columns in (mine, theirs):
        remote(piece, 1, beside, columns).start()
        remote(piece, 2, along, columns).start()
        remote(piece, 5 - last, first, columns).start()
        if columns is mine:
            join(core, 1).start()
            join(core, 0).wait_recv()
    remote(piece, 3, across).start()
    remote(piece, 4 + last, second).start()
    pltpu.make_async_copy(piece, slots.at[0], recv_sems.at[0]).start()
    beside_source, along_source = 4 + column, 4 + row
    beyond = jnp.where(row == 0, above, below)
    join(other, 1).wait_recv()

    for i in range(block):
        own_t[i] = own[i].T

    near, far = 4 + last, 5 - last

    def forward(source):
        @pl.when(beside_source == source)
        def _():
            remote(slots.at[source], 6, beside).start()

        @pl.when(along_source == source)
        def _():
            remote(slots.at[source], 7, along).start()

    def visit(step, carry):
        slot = jnp.where(step == 1, near, jnp.where(step == 4, far, jnp.where(step == 5, 3, step)))
        slot = jnp.where(step == 2, 1, jnp.where(step == 3, 2, slot))

        @pl.when(step != 5)
        def _():
            arrived(slot)

        @pl.when(step == 1)
        def _():
            forward(near)

        @pl.when(step == 4)
        def _():
            forward(far)
            arrived(3)
            remote(slots.at[3], 8, beyond).start()

        to_owner = jnp.where(slot == 0, me, jnp.where(slot == 1, beside, jnp.where(slot == 2, along, across)))
        from_beside = jnp.where(column == 1, beside + CYCLE, beside + aux_count - CYCLE)
        from_along = jnp.where(row == 1, along + CYCLE, along + aux_count - CYCLE)
        from_beyond = jnp.where(row == 1, across + CYCLE, across + aux_count - CYCLE)
        forwarded = jnp.where(slot == 6, from_beside, jnp.where(slot == 7, from_along, from_beyond))
        forwarded = lax.rem(forwarded, aux_count)
        stacked = jnp.where(slot == 4, above, below)
        owner = jnp.where(slot < 4, to_owner, jnp.where(slot < 6, stacked, forwarded))
        for s in range(share):
            pair_energy = occ_energy[owner * block + core * share + s]
            visitor = slots[slot, s]
            vis_t[...] = visitor.T
            for i in range(block):
                energy = occ_energy[me * block + i] + pair_energy
                for t in range(2):
                    rows = slice(t * half, (t + 1) * half)
                    direct = jnp.dot(own_t[i, rows], visitor, preferred_element_type=jnp.float32)
                    swapped = jnp.dot(vis_t[rows], own[i], preferred_element_type=jnp.float32)
                    inverse = 1.0 / (energy - vir_pairs[rows])
                    amp[i, rows] = (direct * inverse).astype(jnp.bfloat16)
                    mix[i, rows] = ((2.0 * direct - swapped) * inverse).astype(jnp.bfloat16)
                acc[i] += lax.dot_general(amp[i], mix[i], NT, preferred_element_type=jnp.float32)
        return carry

    lax.fori_loop(0, slot_count, visit, 0)

    outgoing[...] = acc[:, theirs].astype(bf16)
    swap = pltpu.make_async_remote_copy(
        src_ref=outgoing,
        dst_ref=incoming,
        send_sem=swap_sems.at[0],
        recv_sem=swap_sems.at[1],
        device_id=(me, other),
        device_id_type=MESH,
    )
    swap.start()
    for slot in range(1, slot_count):
        remote(piece, slot, beside).wait_send()
    for chunk in range(chunks):
        give(chunk).wait_send()
    join(other, 0).wait_send()
    join(core, 1).wait_send()
    sent = outbox.at[:, pl.ds(0, norb - block)]
    pltpu.make_async_copy(sent, sent, spread_sems.at[0]).wait()
    swap.wait()
    out_ref[...] = acc[:, mine] + incoming[...].astype(f32)


def shards(ints, occ_coef, vir_coef, occ_energy, vir_energy):
    aux_count = lax.axis_size("aux")
    ao_count = lax.axis_size("ao")
    held, part, nao = ints.shape
    norb, nvir = occ_coef.shape[1], vir_coef.shape[1]
    block, half, naux = norb // aux_count, nvir // ao_count, held * aux_count
    share = block // ao_count
    slot_count = 2 * CYCLE + 1
    groups, chunks = 4, 2
    depth = held // chunks
    f32, bf16 = jnp.float32, jnp.bfloat16
    anywhere = pl.BlockSpec(memory_space=pl.ANY)
    dma = pltpu.SemaphoreType.DMA
    return pl.pallas_call(
        functools.partial(density_kernel, aux_count, share),
        out_shape=jax.ShapeDtypeStruct((block, half, nvir), f32),
        in_specs=[anywhere] * 5,
        out_specs=pl.BlockSpec(memory_space=pltpu.VMEM),
        scratch_shapes=[
            pltpu.VMEM((groups, held // groups * part, nao), bf16),
            pltpu.VMEM((norb, nao), bf16),
            pltpu.VMEM((part, nvir), bf16),
            pltpu.SMEM((norb,), f32),
            pltpu.VMEM((1, nvir), f32),
            pltpu.VMEM((chunks, depth * norb, part), bf16),
            pltpu.VMEM((chunks, depth * norb, half), bf16),
            pltpu.VMEM((chunks, depth * norb, half), bf16),
            pltpu.VMEM((chunks, depth * norb, half), f32),
            pltpu.VMEM((chunks, norb, depth, half), bf16),
            pltpu.VMEM((block, naux, nvir), bf16),
            pltpu.VMEM((slot_count, share, naux, nvir), bf16),
            pltpu.VMEM((block, nvir, naux), bf16),
            pltpu.VMEM((nvir, naux), bf16),
            pltpu.VMEM((nvir, nvir), f32),
            pltpu.VMEM((block, nvir, nvir), bf16),
            pltpu.VMEM((block, nvir, nvir), bf16),
            pltpu.VMEM((block, nvir, nvir), f32),
            pltpu.VMEM((block, half, nvir), bf16),
            pltpu.VMEM((block, half, nvir), bf16),
            dma((groups,)),
            dma((4,)),
            dma((chunks,)),
            dma((chunks,)),
            dma((2,)),
            dma((2, 2)),
            dma((slot_count,)),
            dma((slot_count,)),
            dma((2,)),
        ],
        compiler_params=pltpu.CompilerParams(collective_id=0, has_side_effects=True, vmem_limit_bytes=60 * 2**20),
    )(ints.reshape(held * part, nao), occ_coef.T, vir_coef, occ_energy, vir_energy[None, :])


def solution(mesh):
    return jax.shard_map(
        shards,
        mesh=mesh,
        in_specs=(P("aux", "ao", None), P(), P("ao", None), P(), P()),
        out_specs=P("aux", "ao", None),
        check_vma=False,
    )
```

time: 61.5 us -> 52.4 us (0.85)
  Pallas kernels: 29 us -> 49.9 us
  waiting for transfers between devices: 11.2 us -> 0 us
  starting transfers between devices: 8.78 us -> 0 us
  matrix products: 6.84 us -> 0 us
  blocking collectives: 2.18 us -> 0 us
  local copies, waits for them, and re-layouts: 3.03 us -> 2.26 us
    pallas_call x1, Pallas kernels: 29 us -> 49.9 us  [shards(): pl.pallas_call(functools.partial(density_kernel, aux_count, share), out_s...]
    all_to_all x1 -> x0, waiting for transfers between devices: 10 us -> none  [shards(): lax.all_to_all(summed, 'aux', split_axis=1, concat_axis=0, tiled=True)]
    all_to_all x1 -> x0, starting transfers between devices: 8.22 us -> none  [shards(): lax.all_to_all(summed, 'aux', split_axis=1, concat_axis=0, tiled=True)]
    dot_general x1 -> x0, matrix products: 6.84 us -> none  [shards(): jnp.einsum('qmi,ma->qia', half_ints, vir_coef, preferred_element_type=jnp...]
    all_gather x1 -> x0, blocking collectives: 2.18 us -> none  [shards(): own_block = lax.all_gather(grouped, 'ao', axis=2, tiled=True)]
    ppermute x1 -> x0, waiting for transfers between devices: 1.16 us -> none  [shards(): taken = lax.ppermute(given, 'ao', [(0, 1), (1, 0)])]
    convert_element_type x2 -> x0, local copies, waits for them, and re-layouts: 0.9 us -> none  [the longest x1 0.85 us: shards(): summed = (kept + taken.astype(jnp.float32)).astype(jnp.bfloat16)]
    unnamed x7 -> x1, local copies, waits for them, and re-layouts: 1.97 us -> 2.26 us
  transfers between devices with their start and end apart: 2 -> 0, of which waited for: 2 -> 0; matrix products, arithmetic and copies ran while one was open for 0% -> 0% of each run, Pallas kernels for 0% -> 0%
where the time goes in v2:
time: 52.4 us; the launch traced here: 52.2 us
  Pallas kernels  49.9 us (95%)
  local copies, waits for them, and re-layouts  2.26 us (4%)
    pallas_call x1, Pallas kernels, shards(): pl.pallas_call(functools.partial(density_kernel, aux_count, share), out_s...  49.9 us
    unnamed x1, local copies, waits for them, and re-layouts  2.26 us

profile of v2, /device:TPU:0, one launch (start us, length us, event | category | flops | bytes accessed | tf_op | source)
XLA Modules:
  0.0 52.2 jit_solution(12005936703124213701)
XLA Ops:
  0.0 49.9 %shard_map.55 = f32[2,256,512]{2,1,0:T(8,128)} custom-call(bf16[6144,768]{1,0:T(8,128)(2,1)} %bitcast.3, bf16[32,768]{1,0:T(8,128)(2,1)} %bitcast.4, bf16[384,512]{1,0:T(8,128)(2,1)} %vir_ref.1, f32[32]{0:T(128)} %occ_energy_ref.1, f32[1,512]{1,0:T(1,128)} %bitcast.5), custom_call_target="tpu_custom_call" | custom-call | tf_op jit(solution)/shard_map/pallas_call | solution.py:283
  49.9 2.3 %copy.7 = f32[2,256,512]{2,1,0:T(8,128)} copy(f32[2,256,512]{2,1,0:T(8,128)} %shard_map.55) | data formatting | bytes 2097152

commit v3 on v2

--- a/solution.py
+++ b/solution.py
@@ -40,7 +40,7 @@
     groups, rows_in_group, nao = ints.shape
     chunks, norb, depth, half = outbox.shape
     part = half_ints.shape[2]
-    held = chunks * depth
+    deep = naux // chunks
     slot_count = 2 * CYCLE + 1
     column, row, beside, along, across, above, below, last = places(me, aux_count)
     f32, bf16 = jnp.float32, jnp.bfloat16
@@ -96,15 +96,15 @@
         give(chunk).wait_recv()
         total = kept[chunk] + taken[chunk].astype(f32)
         outbox[chunk] = total.astype(bf16).reshape(norb, depth, half)
-        place = pl.ds(pl.multiple_of(me * held + chunk * depth, depth), depth)
+        place = pl.ds(pl.multiple_of(chunk * deep + me * depth, depth), depth)
 
         def send(step, carry):
             target = lax.rem(me + step, aux_count)
             pltpu.make_async_remote_copy(
                 src_ref=outbox.at[chunk, pl.ds(target * block, block)],
                 dst_ref=own.at[:, place, mine],
-                send_sem=spread_sems.at[0],
-                recv_sem=spread_sems.at[1],
+                send_sem=spread_sems.at[chunks],
+                recv_sem=spread_sems.at[chunk],
                 device_id=(target, core),
                 device_id_type=MESH,
             ).start()
@@ -112,7 +112,7 @@
 
         lax.fori_loop(1, aux_count, send, 0)
         pltpu.make_async_copy(
-            outbox.at[chunk, pl.ds(me * block, block)], own.at[:, place, mine], spread_sems.at[1]
+            outbox.at[chunk, pl.ds(me * block, block)], own.at[:, place, mine], spread_sems.at[chunk]
         ).start()
 
     in_chunk = groups // chunks
@@ -143,81 +143,103 @@
     column_energy = jnp.broadcast_to(vir_energy[...], (lanes, nvir)).T
     vir_pairs[...] = jnp.concatenate([column_energy] * (nvir // lanes), axis=1) + vir_energy[...]
 
-    def remote(source, slot, target, columns=slice(None)):
+    def span(chunk):
+        return pl.ds(chunk * deep, deep)
+
+    def remote(source, slot, target, chunk, columns=slice(None)):
         return pltpu.make_async_remote_copy(
-            src_ref=source.at[:, :, columns],
-            dst_ref=slots.at[slot, :, :, columns],
-            send_sem=send_sems.at[slot],
-            recv_sem=recv_sems.at[slot],
+            src_ref=source.at[:, span(chunk), columns],
+            dst_ref=slots.at[slot, :, span(chunk), columns],
+            send_sem=send_sems.at[slot, chunk],
+            recv_sem=recv_sems.at[slot, chunk],
             device_id=(target, core),
             device_id_type=MESH,
         )
 
-    def arrived(slot):
-        pltpu.make_async_copy(slots.at[slot], slots.at[slot], recv_sems.at[slot]).wait()
-
-    def join(orbital, at):
-        half_block = own.at[pl.ds(orbital * share, share), :, mine]
+    def arrived(slot, chunk):
+        region = slots.at[slot, :, span(chunk)]
+        pltpu.make_async_copy(region, region, recv_sems.at[slot, chunk]).wait()
+
+    def join(orbital, at, chunk):
+        half_block = own.at[pl.ds(orbital * share, share), span(chunk), mine]
         return pltpu.make_async_remote_copy(
             src_ref=half_block,
             dst_ref=half_block,
-            send_sem=join_sems.at[0, at],
-            recv_sem=join_sems.at[1, at],
+            send_sem=join_sems.at[0, at, chunk],
+            recv_sem=join_sems.at[1, at, chunk],
             device_id=(me, other),
             device_id_type=MESH,
         )
 
-    own_half = own.at[:, :, mine]
-    pltpu.make_async_copy(own_half, own_half, spread_sems.at[1]).wait()
-    join(other, 0).start()
     piece = own.at[pl.ds(core * share, share)]
     first = jnp.where(last == 1, below, above)
     second = jnp.where(last == 1, above, below)
-    for columns in (mine, theirs):
-        remote(piece, 1, beside, columns).start()
-        remote(piece, 2, along, columns).start()
-        remote(piece, 5 - last, first, columns).start()
-        if columns is mine:
-            join(core, 1).start()
-            join(core, 0).wait_recv()
-    remote(piece, 3, across).start()
-    remote(piece, 4 + last, second).start()
-    pltpu.make_async_copy(piece, slots.at[0], recv_sems.at[0]).start()
+    for chunk in range(chunks):
+        own_half = own.at[:, span(chunk), mine]
+        pltpu.make_async_copy(own_half, own_half, spread_sems.at[chunk]).wait()
+        join(other, 0, chunk).start()
+        for columns in (mine, theirs):
+            remote(piece, 1, beside, chunk, columns).start()
+            remote(piece, 2, along, chunk, columns).start()
+            remote(piece, 5 - last, first, chunk, columns).start()
+            if columns is mine:
+                join(core, 1, chunk).start()
+                join(core, 0, chunk).wait_recv()
+        remote(piece, 3, across, chunk).start()
+        remote(piece, 4 + last, second, chunk).start()
+        pltpu.make_async_copy(
+            piece.at[:, span(chunk)], slots.at[0, :, span(chunk)], recv_sems.at[0, chunk]
+        ).start()
     beside_source, along_source = 4 + column, 4 + row
     beyond = jnp.where(row == 0, above, below)
-    join(other, 1).wait_recv()
+    for chunk in range(chunks):
+        join(other, 1, chunk).wait_recv()
 
     for i in range(block):
         own_t[i] = own[i].T
 
     near, far = 4 + last, 5 - last
 
-    def forward(source):
+    def forward(source, chunk):
         @pl.when(beside_source == source)
         def _():
-            remote(slots.at[source], 6, beside).start()
+            remote(slots.at[source], 6, beside, chunk).start()
 
         @pl.when(along_source == source)
         def _():
-            remote(slots.at[source], 7, along).start()
+            remote(slots.at[source], 7, along, chunk).start()
 
     def visit(step, carry):
-        slot = jnp.where(step == 1, near, jnp.where(step == 4, far, jnp.where(step == 5, 3, step)))
-        slot = jnp.where(step == 2, 1, jnp.where(step == 3, 2, slot))
-
-        @pl.when(step != 5)
-        def _():
-            arrived(slot)
+        slot = jnp.where(step == 3, near, jnp.where(step == 4, far, jnp.where(step == 5, 3, step)))
 
         @pl.when(step == 1)
         def _():
-            forward(near)
+            arrived(near, 0)
+            forward(near, 0)
+
+        @pl.when(step == 2)
+        def _():
+            arrived(3, 0)
+            remote(slots.at[3], 8, beyond, 0).start()
+            arrived(far, 0)
+            forward(far, 0)
+
+        @pl.when(step == 3)
+        def _():
+            arrived(near, 1)
+            forward(near, 1)
 
         @pl.when(step == 4)
         def _():
-            forward(far)
-            arrived(3)
-            remote(slots.at[3], 8, beyond).start()
+            arrived(3, 1)
+            remote(slots.at[3], 8, beyond, 1).start()
+            arrived(far, 1)
+            forward(far, 1)
+
+        @pl.when((step < 3) | (step > 5))
+        def _():
+            for chunk in range(chunks):
+                arrived(slot, chunk)
 
         to_owner = jnp.where(slot == 0, me, jnp.where(slot == 1, beside, jnp.where(slot == 2, along, across)))
         from_beside = jnp.where(column == 1, beside + CYCLE, beside + aux_count - CYCLE)
@@ -256,13 +278,14 @@
     )
     swap.start()
     for slot in range(1, slot_count):
-        remote(piece, slot, beside).wait_send()
+        for chunk in range(chunks):
+            remote(piece, slot, beside, chunk).wait_send()
     for chunk in range(chunks):
         give(chunk).wait_send()
-    join(other, 0).wait_send()
-    join(core, 1).wait_send()
+        join(other, 0, chunk).wait_send()
+        join(core, 1, chunk).wait_send()
     sent = outbox.at[:, pl.ds(0, norb - block)]
-    pltpu.make_async_copy(sent, sent, spread_sems.at[0]).wait()
+    pltpu.make_async_copy(sent, sent, spread_sems.at[chunks]).wait()
     swap.wait()
     out_ref[...] = acc[:, mine] + incoming[...].astype(f32)
 
@@ -280,6 +303,7 @@
     f32, bf16 = jnp.float32, jnp.bfloat16
     anywhere = pl.BlockSpec(memory_space=pl.ANY)
     dma = pltpu.SemaphoreType.DMA
+    operands = (ints.reshape(held * part, nao), occ_coef.T, vir_coef, occ_energy, vir_energy[None, :])
     return pl.pallas_call(
         functools.partial(density_kernel, aux_count, share),
         out_shape=jax.ShapeDtypeStruct((block, half, nvir), f32),
@@ -310,14 +334,14 @@
             dma((4,)),
             dma((chunks,)),
             dma((chunks,)),
-            dma((2,)),
-            dma((2, 2)),
-            dma((slot_count,)),
-            dma((slot_count,)),
+            dma((chunks + 1,)),
+            dma((2, 2, chunks)),
+            dma((slot_count, chunks)),
+            dma((slot_count, chunks)),
             dma((2,)),
         ],
-        compiler_params=pltpu.CompilerParams(collective_id=0, has_side_effects=True, vmem_limit_bytes=60 * 2**20),
-    )(ints.reshape(held * part, nao), occ_coef.T, vir_coef, occ_energy, vir_energy[None, :])
+        compiler_params=pltpu.CompilerParams(collective_id=0, has_side_effects=True, vmem_limit_bytes=44 * 2**20),
+    )(*(pltpu.with_memory_space_constraint(operand, pltpu.HBM) for operand in operands))
 
 
 def solution(mesh):

time: 52.4 us -> 40.7 us (0.78)
  Pallas kernels: 49.9 us -> 39.6 us
  local copies, waits for them, and re-layouts: 2.26 us -> 0.97 us
    pallas_call x1, Pallas kernels: 49.9 us -> 39.6 us  [shards(): pl.pallas_call(functools.partial(density_kernel, aux_count, share), out_s...]
    unnamed x1, local copies, waits for them, and re-layouts: 2.26 us -> 0.97 us
where the time goes in v3:
time: 40.7 us; the launch traced here: 40.6 us
  Pallas kernels  39.6 us (97%)
  local copies, waits for them, and re-layouts  0.97 us (2%)
    pallas_call x1, Pallas kernels, shards(): pl.pallas_call(functools.partial(density_kernel, aux_count, share), out_s...  39.6 us
    unnamed x1, local copies, waits for them, and re-layouts  0.97 us

profile of v3, /device:TPU:0, one launch (start us, length us, event | category | flops | bytes accessed | tf_op | source)
XLA Modules:
  0.0 40.6 jit_solution(6883964334976910705)
XLA Ops:
  0.0 39.6 %shard_map.55 = f32[2,256,512]{2,1,0:T(8,128)S(1)} custom-call(bf16[6144,768]{1,0:T(8,128)(2,1)} %bitcast.3, bf16[32,768]{1,0:T(8,128)(2,1)} %bitcast.4, bf16[384,512]{1,0:T(8,128)(2,1)} %vir_ref.1, f32[32]{0:T(128)} %occ_energy_ref.1, f32[1,512]{1,0:T(1,128)} %bitcast.5), custom_call_target="tpu_custom_call" | custom-call | tf_op jit(solution)/shard_map/pallas_call | solution.py:307
  39.6 1.0 %copy.7 = f32[2,256,512]{2,1,0:T(8,128)} copy(f32[2,256,512]{2,1,0:T(8,128)S(1)} %shard_map.55) | data formatting | bytes 2097152

commit v4 on v3

--- a/solution.py
+++ b/solution.py
@@ -9,7 +9,6 @@
 
 CYCLE = 4
 MESH = pl.DeviceIdType.MESH
-NT = (((1,), (1,)), ((), ()))
 
 
 def places(me, aux_count):
@@ -29,7 +28,7 @@
 def density_kernel(
     aux_count, share, ints_ref, occ_ref, vir_ref, occ_energy_ref, vir_energy_ref, out_ref,
     ints, occ_t, vir, occ_energy, vir_energy, half_ints, given, taken, kept, outbox, own,
-    slots, own_t, vis_t, vir_pairs, amp, mix, acc, outgoing, incoming,
+    slots, own_t, vir_pairs, amp, mix, acc, outgoing, incoming,
     load_sems, input_sems, give_sems, take_sems, spread_sems, join_sems,
     send_sems, recv_sems, swap_sems,
 ):
@@ -75,6 +74,8 @@
     inputs[0].wait()
     occ = occ_t[...].T
     acc[...] = jnp.zeros_like(acc)
+    amp[block - 1] = jnp.zeros_like(amp[block - 1])
+    mix[block - 1] = jnp.zeros_like(mix[block - 1])
     inputs[1].wait()
     mine = pl.ds(pl.multiple_of(core * half, half), half)
     theirs = pl.ds(pl.multiple_of(other * half, half), half)
@@ -133,7 +134,7 @@
                 pl.semaphore_wait(barrier, aux_count)
             give(chunk).start()
             kept[chunk] = jnp.dot(ordered, vir[:, mine], preferred_element_type=f32)
-        elif chunk > 0:
+        elif chunk > 0 and group % in_chunk == 0:
             spread(chunk - 1)
     spread(chunks - 1)
 
@@ -209,7 +210,26 @@
         def _():
             remote(slots.at[source], 7, along, chunk).start()
 
-    def visit(step, carry):
+    def settle(i, rows=slice(None)):
+        acc[i, rows] += jnp.dot(amp[i, rows], mix[i], preferred_element_type=f32)
+
+    def swap(i):
+        return pltpu.make_async_remote_copy(
+            src_ref=outgoing.at[i],
+            dst_ref=incoming.at[i],
+            send_sem=swap_sems.at[0, i],
+            recv_sem=swap_sems.at[1, i],
+            device_id=(me, other),
+            device_id_type=MESH,
+        )
+
+    def hand_over(i):
+        outgoing[i] = acc[i, theirs].astype(bf16)
+        swap(i).start()
+
+    tiles = [slice(0, half), slice(half, nvir)]
+
+    def visit(step, final=False):
         slot = jnp.where(step == 3, near, jnp.where(step == 4, far, jnp.where(step == 5, 3, step)))
 
         @pl.when(step == 1)
@@ -252,31 +272,26 @@
         for s in range(share):
             pair_energy = occ_energy[owner * block + core * share + s]
             visitor = slots[slot, s]
-            vis_t[...] = visitor.T
             for i in range(block):
                 energy = occ_energy[me * block + i] + pair_energy
-                for t in range(2):
-                    rows = slice(t * half, (t + 1) * half)
-                    direct = jnp.dot(own_t[i, rows], visitor, preferred_element_type=jnp.float32)
-                    swapped = jnp.dot(vis_t[rows], own[i], preferred_element_type=jnp.float32)
-                    inverse = 1.0 / (energy - vir_pairs[rows])
-                    amp[i, rows] = (direct * inverse).astype(jnp.bfloat16)
-                    mix[i, rows] = ((2.0 * direct - swapped) * inverse).astype(jnp.bfloat16)
-                acc[i] += lax.dot_general(amp[i], mix[i], NT, preferred_element_type=jnp.float32)
+                for rows in tiles:
+                    direct = jnp.dot(own_t[i, rows], visitor, preferred_element_type=f32)
+                    amp[i, rows] = (direct * (1.0 / (energy - vir_pairs[rows]))).astype(bf16)
+                settle((i - 1) % block)
+                if final and s == share - 1 and i > 0:
+                    hand_over(i - 1)
+                for rows in tiles:
+                    mix[i, rows] = 2 * amp[i, :, rows].T - amp[i, rows]
+
+    def step_of(step, carry):
+        visit(step)
         return carry
 
-    lax.fori_loop(0, slot_count, visit, 0)
-
-    outgoing[...] = acc[:, theirs].astype(bf16)
-    swap = pltpu.make_async_remote_copy(
-        src_ref=outgoing,
-        dst_ref=incoming,
-        send_sem=swap_sems.at[0],
-        recv_sem=swap_sems.at[1],
-        device_id=(me, other),
-        device_id_type=MESH,
-    )
-    swap.start()
+    lax.fori_loop(0, slot_count - 1, step_of, 0)
+    visit(slot_count - 1, final=True)
+    settle(block - 1, theirs)
+    hand_over(block - 1)
+    settle(block - 1, mine)
     for slot in range(1, slot_count):
         for chunk in range(chunks):
             remote(piece, slot, beside, chunk).wait_send()
@@ -286,8 +301,9 @@
         join(core, 1, chunk).wait_send()
     sent = outbox.at[:, pl.ds(0, norb - block)]
     pltpu.make_async_copy(sent, sent, spread_sems.at[chunks]).wait()
-    swap.wait()
-    out_ref[...] = acc[:, mine] + incoming[...].astype(f32)
+    for i in range(block):
+        swap(i).wait()
+        out_ref[i] = acc[i, mine] + incoming[i].astype(f32)
 
 
 def shards(ints, occ_coef, vir_coef, occ_energy, vir_energy):
@@ -323,7 +339,6 @@
             pltpu.VMEM((block, naux, nvir), bf16),
             pltpu.VMEM((slot_count, share, naux, nvir), bf16),
             pltpu.VMEM((block, nvir, naux), bf16),
-            pltpu.VMEM((nvir, naux), bf16),
             pltpu.VMEM((nvir, nvir), f32),
             pltpu.VMEM((block, nvir, nvir), bf16),
             pltpu.VMEM((block, nvir, nvir), bf16),
@@ -338,7 +353,7 @@
             dma((2, 2, chunks)),
             dma((slot_count, chunks)),
             dma((slot_count, chunks)),
-            dma((2,)),
+            dma((2, block)),
         ],
         compiler_params=pltpu.CompilerParams(collective_id=0, has_side_effects=True, vmem_limit_bytes=44 * 2**20),
     )(*(pltpu.with_memory_space_constraint(operand, pltpu.HBM) for operand in operands))

time: 40.7 us -> 38.9 us (0.956)
  Pallas kernels: 39.6 us -> 37.7 us
    pallas_call x1, Pallas kernels: 39.6 us -> 37.7 us  [shards(): pl.pallas_call(functools.partial(density_kernel, aux_count, share), out_s...]
where the time goes in v4:
time: 38.9 us; the launch traced here: 38.7 us
  Pallas kernels  37.7 us (97%)
  local copies, waits for them, and re-layouts  0.97 us (2%)
    pallas_call x1, Pallas kernels, shards(): pl.pallas_call(functools.partial(density_kernel, aux_count, share), out_s...  37.7 us
    unnamed x1, local copies, waits for them, and re-layouts  0.97 us

profile of v4, /device:TPU:0, one launch (start us, length us, event | category | flops | bytes accessed | tf_op | source)
XLA Modules:
  0.0 38.7 jit_solution(8358174856806681159)
XLA Ops:
  0.0 37.7 %shard_map.55 = f32[2,256,512]{2,1,0:T(8,128)S(1)} custom-call(bf16[6144,768]{1,0:T(8,128)(2,1)} %bitcast.3, bf16[32,768]{1,0:T(8,128)(2,1)} %bitcast.4, bf16[384,512]{1,0:T(8,128)(2,1)} %vir_ref.1, f32[32]{0:T(128)} %occ_energy_ref.1, f32[1,512]{1,0:T(1,128)} %bitcast.5), custom_call_target="tpu_custom_call" | custom-call | tf_op jit(solution)/shard_map/pallas_call | solution.py:323
  37.7 1.0 %copy.7 = f32[2,256,512]{2,1,0:T(8,128)} copy(f32[2,256,512]{2,1,0:T(8,128)S(1)} %shard_map.55) | data formatting | bytes 2097152

commit v5 on v4

--- a/solution.py
+++ b/solution.py
@@ -22,7 +22,8 @@
     above = lax.rem(me + CYCLE, aux_count)
     below = lax.rem(me + aux_count - CYCLE, aux_count)
     last = jnp.where(layer == layers - 1, 1, 0)
-    return column, row, beside, along, across, above, below, last
+    bottom = jnp.where(layer == 0, 1, 0)
+    return column, row, beside, along, across, above, below, bottom, last
 
 
 def density_kernel(
@@ -41,7 +42,7 @@
     part = half_ints.shape[2]
     deep = naux // chunks
     slot_count = 2 * CYCLE + 1
-    column, row, beside, along, across, above, below, last = places(me, aux_count)
+    column, row, beside, along, across, above, below, bottom, last = places(me, aux_count)
     f32, bf16 = jnp.float32, jnp.bfloat16
 
     inputs = [
@@ -173,21 +174,22 @@
         )
 
     piece = own.at[pl.ds(core * share, share)]
-    first = jnp.where(last == 1, below, above)
-    second = jnp.where(last == 1, above, below)
+    first = jnp.where(last == 1, above, below)
+    second = jnp.where(last == 1, below, above)
     for chunk in range(chunks):
         own_half = own.at[:, span(chunk), mine]
         pltpu.make_async_copy(own_half, own_half, spread_sems.at[chunk]).wait()
         join(other, 0, chunk).start()
         for columns in (mine, theirs):
-            remote(piece, 1, beside, chunk, columns).start()
-            remote(piece, 2, along, chunk, columns).start()
-            remote(piece, 5 - last, first, chunk, columns).start()
+            remote(piece, 3, across, chunk, columns).start()
+            remote(piece, 4 + last, first, chunk, columns).start()
             if columns is mine:
                 join(core, 1, chunk).start()
                 join(core, 0, chunk).wait_recv()
-        remote(piece, 3, across, chunk).start()
-        remote(piece, 4 + last, second, chunk).start()
+        remote(piece, 5 - last, second, chunk).start()
+        if chunk == 0:
+            remote(piece, 1, beside, chunk).start()
+            remote(piece, 2, along, chunk).start()
         pltpu.make_async_copy(
             piece.at[:, span(chunk)], slots.at[0, :, span(chunk)], recv_sems.at[0, chunk]
         ).start()
@@ -199,7 +201,7 @@
     for i in range(block):
         own_t[i] = own[i].T
 
-    near, far = 4 + last, 5 - last
+    early, late = 4 + bottom, 5 - bottom
 
     def forward(source, chunk):
         @pl.when(beside_source == source)
@@ -230,33 +232,33 @@
     tiles = [slice(0, half), slice(half, nvir)]
 
     def visit(step, final=False):
-        slot = jnp.where(step == 3, near, jnp.where(step == 4, far, jnp.where(step == 5, 3, step)))
+        slot = jnp.where(step == 1, 3, jnp.where(step == 2, early, jnp.where(step == 3, late, step)))
+        slot = jnp.where(step == 4, 1, jnp.where(step == 5, 2, slot))
 
         @pl.when(step == 1)
         def _():
-            arrived(near, 0)
-            forward(near, 0)
+            for chunk in range(chunks):
+                arrived(3, chunk)
+                remote(slots.at[3], 8, beyond, chunk).start()
+                if chunk == 0:
+                    arrived(early, 0)
+                    forward(early, 0)
+                    arrived(late, 0)
+                    forward(late, 0)
+                    remote(piece, 1, beside, 1).start()
+                    remote(piece, 2, along, 1).start()
 
         @pl.when(step == 2)
         def _():
-            arrived(3, 0)
-            remote(slots.at[3], 8, beyond, 0).start()
-            arrived(far, 0)
-            forward(far, 0)
+            arrived(early, 1)
+            forward(early, 1)
 
         @pl.when(step == 3)
         def _():
-            arrived(near, 1)
-            forward(near, 1)
-
-        @pl.when(step == 4)
-        def _():
-            arrived(3, 1)
-            remote(slots.at[3], 8, beyond, 1).start()
-            arrived(far, 1)
-            forward(far, 1)
-
-        @pl.when((step < 3) | (step > 5))
+            arrived(late, 1)
+            forward(late, 1)
+
+        @pl.when((step < 1) | (step > 3))
         def _():
             for chunk in range(chunks):
                 arrived(slot, chunk)

time: 38.9 us -> 38.7 us (level)
  no operation moved by 1% of the time
where the time goes in v5:
time: 38.7 us; the launch traced here: 38.5 us
  Pallas kernels  37.5 us (97%)
  local copies, waits for them, and re-layouts  0.97 us (3%)
    pallas_call x1, Pallas kernels, shards(): pl.pallas_call(functools.partial(density_kernel, aux_count, share), out_s...  37.5 us
    unnamed x1, local copies, waits for them, and re-layouts  0.97 us

profile of v5, /device:TPU:0, one launch (start us, length us, event | category | flops | bytes accessed | tf_op | source)
XLA Modules:
  0.0 38.5 jit_solution(12055927395697347761)
XLA Ops:
  0.0 37.5 %shard_map.55 = f32[2,256,512]{2,1,0:T(8,128)S(1)} custom-call(bf16[6144,768]{1,0:T(8,128)(2,1)} %bitcast.3, bf16[32,768]{1,0:T(8,128)(2,1)} %bitcast.4, bf16[384,512]{1,0:T(8,128)(2,1)} %vir_ref.1, f32[32]{0:T(128)} %occ_energy_ref.1, f32[1,512]{1,0:T(1,128)} %bitcast.5), custom_call_target="tpu_custom_call" | custom-call | tf_op jit(solution)/shard_map/pallas_call | solution.py:325
  37.5 1.0 %copy.7 = f32[2,256,512]{2,1,0:T(8,128)} copy(f32[2,256,512]{2,1,0:T(8,128)S(1)} %shard_map.55) | data formatting | bytes 2097152

commit v6 on v5

--- a/solution.py
+++ b/solution.py
@@ -27,9 +27,9 @@
 
 
 def density_kernel(
-    aux_count, share, ints_ref, occ_ref, vir_ref, occ_energy_ref, vir_energy_ref, out_ref,
+    aux_count, share, ints_ref, occ_ref, vir_ref, occ_energy_ref, vir_energy_ref, kept_ref, incoming,
     ints, occ_t, vir, occ_energy, vir_energy, half_ints, given, taken, kept, outbox, own,
-    slots, own_t, vir_pairs, amp, mix, acc, outgoing, incoming,
+    slots, own_t, vir_pairs, amp, mix, acc, outgoing,
     load_sems, input_sems, give_sems, take_sems, spread_sems, join_sems,
     send_sems, recv_sems, swap_sems,
 ):
@@ -304,8 +304,9 @@
     sent = outbox.at[:, pl.ds(0, norb - block)]
     pltpu.make_async_copy(sent, sent, spread_sems.at[chunks]).wait()
     for i in range(block):
+        kept_ref[i] = acc[i, mine]
+    for i in range(block):
         swap(i).wait()
-        out_ref[i] = acc[i, mine] + incoming[i].astype(f32)
 
 
 def shards(ints, occ_coef, vir_coef, occ_energy, vir_energy):
@@ -322,11 +323,11 @@
     anywhere = pl.BlockSpec(memory_space=pl.ANY)
     dma = pltpu.SemaphoreType.DMA
     operands = (ints.reshape(held * part, nao), occ_coef.T, vir_coef, occ_energy, vir_energy[None, :])
-    return pl.pallas_call(
+    kept, incoming = pl.pallas_call(
         functools.partial(density_kernel, aux_count, share),
-        out_shape=jax.ShapeDtypeStruct((block, half, nvir), f32),
+        out_shape=[jax.ShapeDtypeStruct((block, half, nvir), kind) for kind in (f32, bf16)],
         in_specs=[anywhere] * 5,
-        out_specs=pl.BlockSpec(memory_space=pltpu.VMEM),
+        out_specs=[pl.BlockSpec(memory_space=pltpu.VMEM)] * 2,
         scratch_shapes=[
             pltpu.VMEM((groups, held // groups * part, nao), bf16),
             pltpu.VMEM((norb, nao), bf16),
@@ -346,7 +347,6 @@
             pltpu.VMEM((block, nvir, nvir), bf16),
             pltpu.VMEM((block, nvir, nvir), f32),
             pltpu.VMEM((block, half, nvir), bf16),
-            pltpu.VMEM((block, half, nvir), bf16),
             dma((groups,)),
             dma((4,)),
             dma((chunks,)),
@@ -359,6 +359,7 @@
         ],
         compiler_params=pltpu.CompilerParams(collective_id=0, has_side_effects=True, vmem_limit_bytes=44 * 2**20),
     )(*(pltpu.with_memory_space_constraint(operand, pltpu.HBM) for operand in operands))
+    return kept + incoming.astype(f32)
 
 
 def solution(mesh):

time: 38.7 us -> 38.8 us (level)
  other arithmetic: 0 us -> 1.15 us
  local copies, waits for them, and re-layouts: 0.97 us -> 0 us
    add x0 -> x1, other arithmetic: none -> 1.15 us  [shards(): return kept + incoming.astype(f32)]
    unnamed x1 -> x0, local copies, waits for them, and re-layouts: 0.97 us -> none
where the time goes in v6:
time: 38.8 us; the launch traced here: 38.6 us
  Pallas kernels  37.5 us (97%)
  other arithmetic  1.15 us (3%)
    pallas_call x1, Pallas kernels, shards(): pl.pallas_call(functools.partial(density_kernel, aux_count, share), out_s...  37.5 us
    add x1, other arithmetic, shards(): return kept + incoming.astype(f32)  1.15 us

profile of v6, /device:TPU:0, one launch (start us, length us, event | category | flops | bytes accessed | tf_op | source)
XLA Modules:
  0.0 38.6 jit_solution(14252107888932795973)
XLA Ops:
  0.0 37.5 %shard_map.55 = (f32[2,256,512]{2,1,0:T(8,128)S(1)}, bf16[2,256,512]{2,1,0:T(8,128)(2,1)S(1)}) custom-call(bf16[6144,768]{1,0:T(8,128)(2,1)} %bitcast.3, bf16[32,768]{1,0:T(8,128)(2,1)} %bitcast.4, bf16[384,512]{1,0:T(8,128)(2,1)} %vir_ref.1, f32[32]{0:T(128)} %occ_energy_ref.1, f32[1,512]{1,0:T(1,128)} %bitcast.5), custom_call_target="tpu_custom_call" | custom-call | tf_op jit(solution)/shard_map/pallas_call | solution.py:326
  37.5 1.1 %convert_add_fusion = f32[2,256,512]{2,1,0:T(8,128)} fusion(f32[2,256,512]{2,1,0:T(8,128)S(1)} %get-tuple-element.7, bf16[2,256,512]{2,1,0:T(8,128)(2,1)S(1)} %get-tuple-element.8), kind=kLoop, calls=%fused_computation | loop fusion | flops 524288 | bytes 2621440 | tf_op jit(solution)/shard_map/add | solution.py:362

commit v7 on v5

--- a/solution.py
+++ b/solution.py
@@ -229,7 +229,7 @@
         outgoing[i] = acc[i, theirs].astype(bf16)
         swap(i).start()
 
-    tiles = [slice(0, half), slice(half, nvir)]
+    tiles = [slice(0, nvir)]
 
     def visit(step, final=False):
         slot = jnp.where(step == 1, 3, jnp.where(step == 2, early, jnp.where(step == 3, late, step)))

time: 38.7 us -> 38.6 us (level)
  no operation moved by 1% of the time
where the time goes in v7:
time: 38.6 us; the launch traced here: 38.5 us
  Pallas kernels  37.5 us (97%)
  local copies, waits for them, and re-layouts  0.97 us (3%)
    pallas_call x1, Pallas kernels, shards(): pl.pallas_call(functools.partial(density_kernel, aux_count, share), out_s...  37.5 us
    unnamed x1, local copies, waits for them, and re-layouts  0.97 us

profile of v7, /device:TPU:0, one launch (start us, length us, event | category | flops | bytes accessed | tf_op | source)
XLA Modules:
  0.0 38.5 jit_solution(14701054161001967121)
XLA Ops:
  0.0 37.5 %shard_map.55 = f32[2,256,512]{2,1,0:T(8,128)S(1)} custom-call(bf16[6144,768]{1,0:T(8,128)(2,1)} %bitcast.3, bf16[32,768]{1,0:T(8,128)(2,1)} %bitcast.4, bf16[384,512]{1,0:T(8,128)(2,1)} %vir_ref.1, f32[32]{0:T(128)} %occ_energy_ref.1, f32[1,512]{1,0:T(1,128)} %bitcast.5), custom_call_target="tpu_custom_call" | custom-call | tf_op jit(solution)/shard_map/pallas_call | solution.py:325
  37.5 1.0 %copy.7 = f32[2,256,512]{2,1,0:T(8,128)} copy(f32[2,256,512]{2,1,0:T(8,128)S(1)} %shard_map.55) | data formatting | bytes 2097152

commit v8 on v5

--- a/solution.py
+++ b/solution.py
@@ -237,16 +237,15 @@
 
         @pl.when(step == 1)
         def _():
-            for chunk in range(chunks):
-                arrived(3, chunk)
-                remote(slots.at[3], 8, beyond, chunk).start()
-                if chunk == 0:
-                    arrived(early, 0)
-                    forward(early, 0)
-                    arrived(late, 0)
-                    forward(late, 0)
-                    remote(piece, 1, beside, 1).start()
-                    remote(piece, 2, along, 1).start()
+            arrived(3, 0)
+            remote(slots.at[3], 8, beyond, 0).start()
+            remote(piece, 1, beside, 1).start()
+            remote(piece, 2, along, 1).start()
+            for source in (early, late):
+                arrived(source, 0)
+                forward(source, 0)
+            arrived(3, 1)
+            remote(slots.at[3], 8, beyond, 1).start()
 
         @pl.when(step == 2)
         def _():

time: 38.7 us -> 38.7 us (level)
  no operation moved by 1% of the time
where the time goes in v8:
time: 38.7 us; the launch traced here: 38.5 us
  Pallas kernels  37.6 us (97%)
  local copies, waits for them, and re-layouts  0.97 us (3%)
    pallas_call x1, Pallas kernels, shards(): pl.pallas_call(functools.partial(density_kernel, aux_count, share), out_s...  37.6 us
    unnamed x1, local copies, waits for them, and re-layouts  0.97 us

profile of v8, /device:TPU:0, one launch (start us, length us, event | category | flops | bytes accessed | tf_op | source)
XLA Modules:
  0.0 38.5 jit_solution(10492278495401307544)
XLA Ops:
  0.0 37.6 %shard_map.55 = f32[2,256,512]{2,1,0:T(8,128)S(1)} custom-call(bf16[6144,768]{1,0:T(8,128)(2,1)} %bitcast.3, bf16[32,768]{1,0:T(8,128)(2,1)} %bitcast.4, bf16[384,512]{1,0:T(8,128)(2,1)} %vir_ref.1, f32[32]{0:T(128)} %occ_energy_ref.1, f32[1,512]{1,0:T(1,128)} %bitcast.5), custom_call_target="tpu_custom_call" | custom-call | tf_op jit(solution)/shard_map/pallas_call | solution.py:324
  37.6 1.0 %copy.7 = f32[2,256,512]{2,1,0:T(8,128)} copy(f32[2,256,512]{2,1,0:T(8,128)S(1)} %shard_map.55) | data formatting | bytes 2097152
